TPU v7x, 32 devices: a whole 2x2x4 slice. The times are simulated.
32 devices in a mesh: dp: 8 (over y, x, core), section: 4 (over z).
Axes of the slice: x: 2, y: 2, z: 4, core: 2. Of those that a mesh axis runs over, the one named last changes fastest.
Arguments:
- activations: bfloat16 [4, 512, 2048], P(None, 'dp'), may hold values from -6 to 6
- cotangent: bfloat16 [4, 512, 2048], P(None, 'dp'), may hold values from -6 to 6
- weight: bfloat16 [4, 2048, 2048], P('section', 'dp'), may hold values from -0.125 to 0.125
- norm_gain: float32 [4, 2048], P('section'), may hold values from 0.1 to 1.9
- pair_mask: int32 [4, 512, 2048], P('section'), may hold values from 0 to 5, as said below
- earlier_mask: int32 [4, 512, 2048], P('section', 'dp'), may hold values from 0 to 5, as said below
Outputs:
- weight_grad: float32 [4, 2048, 2048], P('section', 'dp')
- flip_count: int32 [4], P('section')
Inputs may be any that keep to these rules, and one draw needn't show every extreme that they name: `pair_mask`: pair number of each group of four consecutive rows and each column; pairs numbered (0,1), (0,2), (0,3), (1,2), (1,3), (2,3). `earlier_mask`: pair numbers of the previous step, numbered likewise.
All inputs are finite; a program needn't handle non-finite values.
Results may differ from a plain program's by a relative error of at most 0.02.
Values may be sent and summed in bfloat16 or wider, within the bound.
A program may use at most 64 MiB of HBM per device.

v0:
```python
import functools
import math

import jax
import jax.numpy as jnp
from jax import lax
from jax.experimental import pallas as pl
from jax.experimental.pallas import tpu as pltpu
from jax.sharding import PartitionSpec as P

epsilon = 1e-06
decay_rate = 4.0
half_root = 0.7071067811865476
density_scale = 0.3989422804014327
first_table = (0, 0, 0, 1, 1, 2)
second_table = (1, 2, 3, 2, 3, 3)


def shifted(block, axis, distance):
    devices = range(lax.axis_size(axis))
    route = [(i - distance, i) for i in devices if i - distance in devices]
    return lax.ppermute(block, axis, route)


def pair_ends(indices):
    leading = jnp.zeros_like(indices)
    trailing = jnp.zeros_like(indices)
    for pair_index in range(6):
        matches = indices == pair_index
        leading = jnp.where(matches, first_table[pair_index], leading)
        trailing = jnp.where(matches, second_table[pair_index], trailing)
    return (leading, trailing)


def kept_positions(indices):
    leading, trailing = pair_ends(indices)
    groups, columns = indices.shape
    positions = lax.broadcasted_iota(jnp.int32, (groups, 4, columns), 1)
    kept_mask = (positions == leading[:, None, :]) | (positions == trailing[:, None, :])
    return kept_mask.reshape(groups * 4, columns)


def section_forward(inputs, masked, gain_row):
    values = inputs.astype(jnp.float32)
    norm_scale = lax.rsqrt(jnp.mean(values * values, axis=-1, keepdims=True) + epsilon)
    normed = (values * norm_scale * gain_row).astype(jnp.bfloat16)
    preact = jnp.dot(normed, masked, preferred_element_type=jnp.float32)
    normal_cdf = 0.5 * (1.0 + lax.erf(preact * half_root))
    outputs = (values + preact * normal_cdf).astype(jnp.bfloat16)
    return (normed, preact, outputs)


def section_backward(inputs, preact, upstream, masked, gain_row):
    values = inputs.astype(jnp.float32)
    norm_scale = lax.rsqrt(jnp.mean(values * values, axis=-1, keepdims=True) + epsilon)
    normal_cdf = 0.5 * (1.0 + lax.erf(preact * half_root))
    normal_pdf = jnp.exp(-0.5 * preact * preact) * density_scale
    upstream_f = upstream.astype(jnp.float32)
    grad_pre = (upstream_f * (normal_cdf + preact * normal_pdf)).astype(jnp.bfloat16)
    grad_normed = lax.dot_general(
        grad_pre, masked, (((1,), (1,)), ((), ())), preferred_element_type=jnp.float32
    )
    scaled_grad = grad_normed * gain_row
    grad_input = norm_scale * scaled_grad - values * norm_scale**3 * jnp.mean(
        scaled_grad * values, axis=-1, keepdims=True
    )
    return (grad_pre, (upstream_f + grad_input).astype(jnp.bfloat16))


def write_slot(buffer, new_value, slot_index, is_live):
    old_value = lax.dynamic_index_in_dim(buffer, slot_index, 0, keepdims=False)
    chosen = jnp.where(is_live, new_value, old_value)
    return lax.dynamic_update_index_in_dim(buffer, chosen, slot_index, 0)


def body(activations, cotangent, weight, norm_gain, pair_mask, earlier_mask):
    section_count = lax.axis_size("section")
    replica_count = lax.axis_size("dp")
    section_index = lax.axis_index("section")
    replica_index = lax.axis_index("dp")
    micro_count, row_count, model_width = activations.shape
    shard_rows = weight.shape[1]
    groups = shard_rows // 4
    own_weight = weight[0]
    gain_row = norm_gain[0]
    own_pairs = lax.dynamic_slice_in_dim(pair_mask[0], replica_index * groups, groups, 0)
    own_kept = kept_positions(own_pairs)
    earlier_kept = kept_positions(earlier_mask[0])
    flip_local = jnp.sum(own_kept != earlier_kept).reshape(1)
    flip_sum = lax.psum(flip_local, "dp")
    masked_shard = jnp.where(own_kept, own_weight, jnp.zeros_like(own_weight))
    masked = lax.all_gather(masked_shard, "dp", axis=0, tiled=True)
    tick_count = micro_count + section_count - 1
    act_zeros = jnp.zeros((micro_count, row_count, model_width), jnp.bfloat16)
    stored = (act_zeros,)

    def forward_tick(tick_index, state_tuple):
        received, buffers = state_tuple
        micro_index = tick_index - section_index
        is_live = (micro_index >= 0) & (micro_index < micro_count)
        slot_index = jnp.clip(micro_index, 0, micro_count - 1)
        fresh_rows = lax.dynamic_index_in_dim(activations, slot_index, 0, keepdims=False)
        current = jnp.where(section_index == 0, fresh_rows, received)
        normed, preact, outputs = section_forward(current, masked, gain_row)
        results = (current, normed, preact)
        buffers = tuple(
            (
                write_slot(buffer, update, slot_index, is_live)
                for buffer, update in zip(buffers, results)
            )
        )
        received = shifted(outputs, "section", 1)
        return (received, buffers)

    start_rows = jnp.zeros((row_count, model_width), jnp.bfloat16)
    received, stored = lax.fori_loop(0, tick_count, forward_tick, (start_rows, stored))

    def backward_tick(tick_index, state_tuple):
        received, grad_buffer, normed_buffer = state_tuple
        micro_index = tick_index - (section_count - 1 - section_index)
        is_live = (micro_index >= 0) & (micro_index < micro_count)
        slot_index = jnp.clip(micro_index, 0, micro_count - 1)
        fresh_rows = lax.dynamic_index_in_dim(cotangent, slot_index, 0, keepdims=False)
        upstream = jnp.where(section_index == section_count - 1, fresh_rows, received)
        inputs = lax.dynamic_index_in_dim(stored[0], slot_index, 0, keepdims=False)
        normed, preact, unused = section_forward(inputs, masked, gain_row)
        normed_buffer = write_slot(normed_buffer, normed, slot_index, is_live)
        grad_pre, grad_input = section_backward(inputs, preact, upstream, masked, gain_row)
        grad_buffer = write_slot(grad_buffer, grad_pre, slot_index, is_live)
        received = shifted(grad_input, "section", -1)
        return (received, grad_buffer, normed_buffer)

    received, grad_buffer, normed_buffer = lax.fori_loop(
        0, tick_count, backward_tick, (start_rows, act_zeros, act_zeros)
    )
    flat_normed = normed_buffer.reshape(micro_count * row_count, model_width)
    flat_grad = grad_buffer.reshape(micro_count * row_count, model_width)
    summed = lax.psum_scatter(
        lax.dot_general(
            flat_normed, flat_grad, (((0,), (0,)), ((), ())), preferred_element_type=jnp.float32
        ).astype(jnp.bfloat16),
        "dp",
        scatter_dimension=0,
        tiled=True,
    ).astype(jnp.float32)
    token_total = micro_count * row_count * replica_count
    dense_part = summed / math.sqrt(token_total)
    decay_part = jnp.where(own_kept, 0.0, own_weight.astype(jnp.float32))
    gradient = dense_part + decay_rate * decay_part
    return (gradient[None], flip_sum)


HALVES = (0, 1)


def pick_chunk(rows):
    return 32 if rows % 32 == 0 else 16


def fused_fits(mesh, activations, weight):
    replicas, sections = mesh.shape["dp"], mesh.shape["section"]
    micro, batch, width = activations.shape
    shard_rows = weight.shape[1] // replicas
    rows = micro * batch // replicas
    gathered = replicas // 2 * rows * width * 2
    return (
        replicas % 2 == 0
        and replicas == 2 * len(HALVES) ** 2
        and sections > 1
        and shard_rows % 128 == 0
        and rows % 16 == 0
        and width % 512 == 0
        and gathered + 3 * width * width * 2 < 40 * 2**20
    )


def spread_matrix(count, transposed):
    groups = count // 4
    rows = lax.broadcasted_iota(jnp.int32, (count, count), 1 if transposed else 0)
    columns = lax.broadcasted_iota(jnp.int32, (count, count), 0 if transposed else 1)
    place = sum((columns >= groups * j).astype(jnp.int32) for j in (1, 2, 3))
    hit = rows == 4 * (columns - groups * place) + place
    return jnp.where(hit, 1.0, 0.0).astype(jnp.bfloat16)


def fused_kernel(
    chunk, tokens, act, cot, weight, gain, pairs_hbm, earlier, out, flips,
    packed, full, hidden, normed, deriv, outgoing, upstream, downstream, grads, terms,
    scaled, partial, incoming, counts, pairs, own_pairs, load_sem, row_sem,
    pack_send, pack_recv, relay_send, relay_recv, fwd_send, fwd_recv, bwd_send, bwd_recv,
    term_send, term_recv, grad_send, grad_recv, part_send, part_recv, flip_send, flip_recv, pair_sem,
):
    section = lax.axis_index("section")
    sections = lax.axis_size("section")
    me = lax.axis_index("dp")
    chips = lax.axis_size("dp") // 2
    chip = lax.div(me, 2)
    core = lax.rem(me, 2)
    sibling = 2 * chip + 1 - core
    last = sections - 1
    shard_rows, width = weight.shape
    groups = shard_rows // 4
    rows = hidden.shape[0]
    steps = rows // chunk
    tile = 512
    tiles = width // tile
    across = chip + 1 - 2 * lax.rem(chip, 2)
    along_y = lax.rem(chip + 2, chips)
    corner = lax.rem(across + 2, chips)
    near = (across, along_y)
    own_columns = pl.multiple_of(chip * 2 * shard_rows, 2 * shard_rows)

    def peer_chip(k):
        return lax.rem(chip + k, chips)

    def at_dp(index):
        return {"dp": index}

    def remote(src, dst, send, recv, where):
        return pltpu.make_async_remote_copy(
            src_ref=src, dst_ref=dst, send_sem=send, recv_sem=recv,
            device_id=where, device_id_type=pl.DeviceIdType.MESH,
        )

    barrier = pltpu.get_barrier_semaphore()

    def greet(where):
        pl.semaphore_signal(barrier, inc=1, device_id=where, device_id_type=pl.DeviceIdType.MESH)

    for k in range(1, chips):
        greet(at_dp(2 * peer_chip(k) + core))
    greet(at_dp(sibling))

    @pl.when(section > 0)
    def _():
        greet({"section": section - 1})

    @pl.when(section < last)
    def _():
        greet({"section": section + 1})

    own_load = pltpu.make_async_copy(
        pairs_hbm.at[pl.ds(pl.multiple_of(me * groups, groups), groups), :], own_pairs, load_sem.at[0]
    )
    own_load.start()
    all_load = pltpu.make_async_copy(pairs_hbm, pairs, load_sem.at[1])
    all_load.start()
    micro_rows = act.shape[1]

    def row_loads(source, target):
        return [
            pltpu.make_async_copy(source.at[m], target.at[pl.ds(m * micro_rows, micro_rows)], row_sem.at[m])
            for m in range(act.shape[0])
        ]

    @pl.when(section == 0)
    def _():
        for load in row_loads(act, hidden):
            load.start()

    @pl.when(section == last)
    def _():
        for load in row_loads(cot, upstream):
            load.start()

    own_load.wait()
    gather_rows = spread_matrix(shard_rows, True)
    for t in range(tiles):
        cols = slice(t * tile, (t + 1) * tile)
        split = jnp.dot(gather_rows, weight[:, cols], preferred_element_type=jnp.float32)
        w0, w1, w2, w3 = (split[j * groups:(j + 1) * groups] for j in range(4))
        p = own_pairs[:, cols]
        first = jnp.where(p <= 2, w0, jnp.where(p <= 4, w1, w2))
        second = jnp.where(p == 0, w1, jnp.where((p == 1) | (p == 3), w2, w3))
        packed[me, 0:groups, cols] = first.astype(jnp.bfloat16)
        packed[me, groups:2 * groups, cols] = second.astype(jnp.bfloat16)

    pl.semaphore_wait(barrier, chips + (section > 0).astype(jnp.int32) + (section < last).astype(jnp.int32))

    def half_rows(h):
        return pl.ds(h * groups, groups)

    def pack_copy(way, source, h, route):
        slot = packed.at[2 * source + core, half_rows(h)]
        return remote(slot, slot, pack_send.at[route, h], pack_recv.at[source, h], at_dp(2 * near[way] + core))

    def pack_own(way, h):
        return pack_copy(way, chip, h, way)

    def pack_onward(way):
        return pack_copy(1 - way, near[way], way, 2)

    def pack_arrival(source, h):
        return pack_copy(0, source, h, 0)

    def relay_copy(source, parity):
        slot = packed.at[2 * source + parity]
        return remote(slot, slot, relay_send.at[source], relay_recv.at[source], at_dp(sibling))

    for h in HALVES:
        for way in (0, 1):
            pack_own(way, h if way == 0 else 1 - h).start()
    relay_copy(chip, core).start()

    p = own_pairs[...]
    q = earlier[...]
    changed = jnp.where(p == q, 0, jnp.where(p + q == 5, 4, 2))
    total = jnp.zeros((8, 128), jnp.int32)
    for a in range(groups // 8):
        for b in range(width // 128):
            total = total + changed[a * 8:(a + 1) * 8, b * 128:(b + 1) * 128]
    counts[chip] = total

    def flip_copy(k, source):
        slot = counts.at[source]
        return remote(slot, slot, flip_send.at[k], flip_recv.at[source], at_dp(2 * peer_chip(k) + core))

    for k in range(1, chips):
        flip_copy(k, chip).start()

    spread_rows = spread_matrix(shard_rows, False)

    def unpack(owner):
        owned = pl.multiple_of(owner * groups, groups)
        target = pl.multiple_of(owner * shard_rows, shard_rows)
        for t in range(tiles):
            cols = slice(t * tile, (t + 1) * tile)
            p = pairs[pl.ds(owned, groups), cols]
            v0 = packed[owner, 0:groups, cols].astype(jnp.float32)
            v1 = packed[owner, groups:2 * groups, cols].astype(jnp.float32)
            zero = jnp.zeros_like(v0)
            parts = (
                jnp.where(p <= 2, v0, zero),
                jnp.where((p == 3) | (p == 4), v0, jnp.where(p == 0, v1, zero)),
                jnp.where(p == 5, v0, jnp.where((p == 1) | (p == 3), v1, zero)),
                jnp.where((p == 2) | (p >= 4), v1, zero),
            )
            stacked = jnp.concatenate(parts, axis=0).astype(jnp.bfloat16)
            spread = jnp.dot(spread_rows, stacked, preferred_element_type=jnp.float32)
            full[pl.ds(target, shard_rows), cols] = spread.astype(jnp.bfloat16)

    all_load.wait()

    def unpack_two(first, second):
        def one(k, carry):
            unpack(jnp.where(k == 0, first, second))
            return carry

        lax.fori_loop(0, 2, one, 0)

    relay_copy(chip, 1 - core).wait_recv()
    unpack_two(2 * chip + core, 2 * chip + 1 - core)
    for way in (0, 1):
        pack_arrival(near[way], way).wait_recv()
        pack_onward(way).start()
    for way in (0, 1):
        pack_arrival(near[way], 1 - way).wait_recv()
        relay_copy(near[way], core).start()
    unpack_two(2 * across + core, 2 * along_y + core)
    for way in (0, 1):
        relay_copy(near[way], 1 - core).wait_recv()
    unpack_two(2 * across + 1 - core, 2 * along_y + 1 - core)
    for h in HALVES:
        pack_arrival(corner, h).wait_recv()
    relay_copy(corner, core).start()
    unpack_two_first = 2 * corner + core
    relay_copy(corner, 1 - core).wait_recv()
    unpack_two(unpack_two_first, 2 * corner + 1 - core)

    @pl.when(section == 0)
    def _():
        for load in row_loads(act, hidden):
            load.wait()

    @pl.when(section == last)
    def _():
        for load in row_loads(cot, upstream):
            load.wait()

    def span(i):
        return pl.ds(pl.multiple_of(i * chunk, chunk), chunk)

    def fwd_copy(i):
        return remote(outgoing.at[span(i)], hidden.at[span(i)], fwd_send.at[i], fwd_recv.at[i], {"section": section + 1})

    def fwd_arrival(i):
        return remote(outgoing.at[span(i)], hidden.at[span(i)], fwd_send.at[i], fwd_recv.at[i], {"section": section})

    def bwd_copy(i):
        return remote(downstream.at[span(i)], upstream.at[span(i)], bwd_send.at[i], bwd_recv.at[i], {"section": section - 1})

    def bwd_arrival(i):
        return remote(downstream.at[span(i)], upstream.at[span(i)], bwd_send.at[i], bwd_recv.at[i], {"section": section})

    def term_copy(k, i):
        peer = peer_chip(k)
        wanted = pl.ds(pl.multiple_of(peer * 2 * shard_rows, 2 * shard_rows), 2 * shard_rows)
        return remote(
            normed.at[span(i), wanted], terms.at[chip, span(i)],
            term_send.at[k, i], term_recv.at[chip, i], at_dp(2 * peer + core),
        )

    def grad_copy(way, source, h, route, i):
        slot = grads.at[source, span(i), pl.ds(h * (width // 2), width // 2)]
        return remote(
            slot, slot, grad_send.at[route * 2 + h, i], grad_recv.at[source * 2 + h, i], at_dp(2 * near[way] + core)
        )

    def grad_own(way, h, i):
        return grad_copy(way, chip, h, way, i)

    def grad_onward(way, i):
        return grad_copy(1 - way, near[way], way, 2, i)

    def grad_arrival(source, h, i):
        return grad_copy(0, source, h, 0, i)

    def pass_on(i):
        for way in (0, 1):
            grad_arrival(near[way], way, i).wait_recv()
            grad_onward(way, i).start()

    def forward(i):
        @pl.when(section > 0)
        def _():
            fwd_arrival(i).wait_recv()

        values = hidden[span(i)].astype(jnp.float32)
        scale = lax.rsqrt(jnp.mean(values * values, axis=-1, keepdims=True) + epsilon)
        rounded = (values * scale * gain[...]).astype(jnp.bfloat16)
        normed[span(i)] = rounded
        for t in range(tiles):
            cols = slice(t * tile, (t + 1) * tile)
            preact = jnp.dot(rounded, full[:, cols], preferred_element_type=jnp.float32)
            cdf = 0.5 * (1.0 + lax.erf(preact * half_root))
            pdf = jnp.exp(-0.5 * preact * preact) * density_scale
            deriv[span(i), cols] = cdf + preact * pdf
            outgoing[span(i), cols] = (values[:, cols] + preact * cdf).astype(jnp.bfloat16)

        @pl.when(section < last)
        def _():
            fwd_copy(i).start()

        terms[chip, span(i)] = normed[span(i), pl.ds(own_columns, 2 * shard_rows)]
        for k in range(1, chips):
            term_copy(k, i).start()

    lag = min(2, steps)

    def backward(i):
        @pl.when(section < last)
        def _():
            bwd_arrival(i).wait_recv()

        above = upstream[span(i)].astype(jnp.float32)
        grad_pre = (above * deriv[span(i)]).astype(jnp.bfloat16)
        grads[chip, span(i)] = grad_pre
        for h in HALVES:
            for way in (0, 1):
                grad_own(way, h if way == 0 else 1 - h, i).start()

        @pl.when(i >= lag)
        def _():
            pass_on(i - lag)

        @pl.when(section > 0)
        def _():
            values = hidden[span(i)].astype(jnp.float32)
            scale = lax.rsqrt(jnp.mean(values * values, axis=-1, keepdims=True) + epsilon)
            along = jnp.zeros((chunk, 1), jnp.float32)
            for t in range(tiles):
                cols = slice(t * tile, (t + 1) * tile)
                piece = lax.dot_general(
                    grad_pre, full[cols, :], (((1,), (1,)), ((), ())), preferred_element_type=jnp.float32
                ) * gain[:, cols]
                scaled[:, cols] = piece
                along = along + jnp.sum(piece * values[:, cols], axis=-1, keepdims=True)
            pull = scale * scale * scale * (along / width)
            result = upstream[span(i)].astype(jnp.float32) + scale * scaled[...] - values * pull
            downstream[span(i)] = result.astype(jnp.bfloat16)
            bwd_copy(i).start()

    def step(k, carry):
        at_last = (section == last).astype(jnp.int32)
        half = lax.div(k, 2)
        goes_back = at_last * lax.rem(k, 2) + (1 - at_last) * lax.div(k, steps)
        index = at_last * half + (1 - at_last) * lax.rem(k, steps)

        @pl.when(goes_back == 0)
        def _():
            forward(index)

        @pl.when(goes_back == 1)
        def _():
            backward(index)

        return carry

    lax.fori_loop(0, 2 * steps, step, 0)

    def arrivals(i, carry):
        for k in range(1, chips):
            source = peer_chip(k)
            remote(
                terms.at[source, span(i)], terms.at[source, span(i)],
                term_send.at[k, i], term_recv.at[source, i], at_dp(me),
            ).wait_recv()
        for way in (0, 1):
            grad_arrival(near[way], 1 - way, i).wait_recv()
        for h in HALVES:
            grad_arrival(corner, h, i).wait_recv()
        return carry

    for i in range(steps - lag, steps):
        pass_on(i)

    lax.fori_loop(0, steps, arrivals, 0)

    def product(half, cols):
        left = pl.ds(pl.multiple_of(half * shard_rows, shard_rows), shard_rows)
        total = jnp.zeros((shard_rows, tile), jnp.float32)
        for c in range(chips):
            total = total + lax.dot_general(
                terms[c, :, left], grads[c, :, cols], (((0,), (0,)), ((), ())), preferred_element_type=jnp.float32
            )
        return total

    def part_copy(t):
        return remote(partial.at[t], incoming.at[t], part_send.at[t], part_recv.at[t], at_dp(sibling))

    for t in range(tiles):
        partial[t] = product(1 - core, slice(t * tile, (t + 1) * tile)).astype(jnp.bfloat16)
        part_copy(t).start()
    own_rows = pl.ds(pl.multiple_of(me * shard_rows, shard_rows), shard_rows)
    for t in range(tiles):
        cols = slice(t * tile, (t + 1) * tile)
        pruned = weight[:, cols].astype(jnp.float32) - full[own_rows, cols].astype(jnp.float32)
        out[:, cols] = product(core, cols) * (1.0 / math.sqrt(tokens)) + decay_rate * pruned

    for k in range(1, chips):
        flip_copy(k, peer_chip(k)).wait_recv()
    total = counts[0]
    for c in range(1, chips):
        total = total + counts[c]
    counts[chips] = total
    pair_copy = remote(counts.at[chips], counts.at[chips + 1], pair_sem.at[0], pair_sem.at[1], at_dp(sibling))
    pair_copy.start()

    for t in range(tiles):
        cols = slice(t * tile, (t + 1) * tile)
        part_copy(t).wait_recv()
        out[:, cols] = out[:, cols] + incoming[t].astype(jnp.float32) * (1.0 / math.sqrt(tokens))
    pair_copy.wait_recv()
    flips[...] = counts[chips] + counts[chips + 1]

    pair_copy.wait_send()
    for t in range(tiles):
        part_copy(t).wait_send()
    for k in range(1, chips):
        flip_copy(k, chip).wait_send()

    for way in (0, 1):
        pack_onward(way).wait_send()
        for h in HALVES:
            pack_own(way, h).wait_send()
    for c in range(chips):
        relay_copy(c, core).wait_send()

    def drain(i, carry):
        for k in range(1, chips):
            term_copy(k, i).wait_send()
        for way in (0, 1):
            grad_onward(way, i).wait_send()
            for h in HALVES:
                grad_own(way, h, i).wait_send()

        @pl.when(section < last)
        def _():
            fwd_copy(i).wait_send()

        @pl.when(section > 0)
        def _():
            bwd_copy(i).wait_send()

        return carry

    lax.fori_loop(0, steps, drain, 0)


def fused_body(activations, cotangent, weight, norm_gain, pair_mask, earlier_mask):
    replicas = lax.axis_size("dp")
    chips = replicas // 2
    micro, micro_rows, width = activations.shape
    shard_rows = weight.shape[1]
    groups = shard_rows // 4
    rows = micro * micro_rows
    chunk = pick_chunk(rows)
    steps = rows // chunk
    tile = 512
    tiles = width // tile
    bf, f32 = jnp.bfloat16, jnp.float32
    dma = pltpu.SemaphoreType.DMA
    vmem = pl.BlockSpec(memory_space=pltpu.VMEM)
    hbm = pl.BlockSpec(memory_space=pl.ANY)
    gradient, flips = pl.pallas_call(
        functools.partial(fused_kernel, chunk, rows * replicas),
        out_shape=(
            jax.ShapeDtypeStruct((shard_rows, width), f32),
            jax.ShapeDtypeStruct((8, 128), jnp.int32),
        ),
        in_specs=[hbm, hbm, vmem, vmem, hbm, vmem],
        out_specs=(vmem, vmem),
        scratch_shapes=[
            pltpu.VMEM((replicas, 2 * groups, width), bf),
            pltpu.VMEM((width, width), bf),
            pltpu.VMEM((rows, width), bf),
            pltpu.VMEM((rows, width), bf),
            pltpu.VMEM((rows, width), f32),
            pltpu.VMEM((rows, width), bf),
            pltpu.VMEM((rows, width), bf),
            pltpu.VMEM((rows, width), bf),
            pltpu.VMEM((chips, rows, width), bf),
            pltpu.VMEM((chips, rows, 2 * shard_rows), bf),
            pltpu.VMEM((chunk, width), f32),
            pltpu.VMEM((tiles, shard_rows, tile), bf),
            pltpu.VMEM((tiles, shard_rows, tile), bf),
            pltpu.VMEM((chips + 2, 8, 128), jnp.int32),
            pltpu.VMEM((width // 4, width), jnp.int32),
            pltpu.VMEM((groups, width), jnp.int32),
            dma((2,)), dma((micro,)),
            dma((3, 2)), dma((chips, 2)), dma((chips,)), dma((chips,)),
            dma((steps,)), dma((steps,)), dma((steps,)), dma((steps,)),
            dma((chips, steps)), dma((chips, steps)), dma((6, steps)), dma((2 * chips, steps)),
            dma((tiles,)), dma((tiles,)), dma((chips,)), dma((chips,)), dma((2,)),
        ],
        compiler_params=pltpu.CompilerParams(
            collective_id=0, has_side_effects=True, vmem_limit_bytes=60 * 2**20
        ),
        name="fused_step",
    )(
        activations, cotangent, weight[0], norm_gain, pair_mask[0], earlier_mask[0],
    )
    return (gradient[None], jnp.sum(flips).reshape(1))


def solution(mesh):
    placed = (
        P(None, "dp", None),
        P(None, "dp", None),
        P("section", "dp", None),
        P("section", None),
        P("section", None, None),
        P("section", "dp", None),
    )

    def step(*arrays):
        chosen = fused_body if fused_fits(mesh, arrays[0], arrays[2]) else body
        return jax.shard_map(
            chosen,
            mesh=mesh,
            in_specs=placed,
            out_specs=(P("section", "dp", None), P("section")),
            check_vma=False,
        )(*arrays)

    return step
```

profile of v0, /device:TPU:0, one launch (start us, length us, event | category | flops | bytes accessed | tf_op | source)
XLA Modules:
  0.0 123.8 jit_solution(14115394966252993334)
XLA Ops:
  0.6 118.7 %fused_step.1 = (f32[256,2048]{1,0:T(8,128)}, s32[8,128]{1,0:T(8,128)}) custom-call(bf16[4,64,2048]{2,1,0:T(8,128)(2,1)} %act.1, bf16[4,64,2048]{2,1,0:T(8,128)(2,1)} %cot.1, bf16[256,2048]{1,0:T(8,128)(2,1)} %bitcast.7, f32[1,2048]{1,0:T(1,128)} %gain.1, s32[512,2048]{1,0:T(8,128)} %bitcast.5, s32[64,2048]{1,0:T(8,128)} %bitcast.8), custom_call_target="tpu_custom_call" | custom-call | tf_op jit(solution)/shard_map/fused_step/pallas_call | solution.py:605
  119.3 1.3 %reduce_sum.9 = s32[]{:T(128)} reduce(s32[8,128]{1,0:T(8,128)} %get-tuple-element.5, s32[]{:T(128)} %constant.0.clone.1), dimensions={0,1}, to_apply=%region_0.0 | reduce | flops 1023 | bytes 4104 | tf_op jit(solution)/shard_map/reduce_sum | solution.py:643
  120.6 3.1 %copy.9 = f32[1,256,2048]{2,1,0:T(8,128)} copy(f32[1,256,2048]{2,1,0:T(8,128)} %bitcast.6) | data formatting | bytes 4194304
where the time goes:
time: 124 us
  Pallas kernels  119 us (96%)
  local copies, waits for them, and re-layouts  3.13 us (3%)
  other arithmetic  1.32 us (1%)
    pallas_call x1, Pallas kernels, fused_body(): pl.pallas_call(functools.partial(fused_kernel, chunk, rows * replicas), o...  119 us
    unnamed x1, local copies, waits for them, and re-layouts  3.13 us

commit v1 on v0

--- a/solution.py
+++ b/solution.py
@@ -153,8 +153,50 @@
 HALVES = (0, 1)
 
 
-def pick_chunk(rows):
-    return 32 if rows % 32 == 0 else 16
+SMALL = 16
+BIG = 32
+SMALL_COUNT = 4
+FAR_LAG = 3
+FILL = 128
+LATE_ROWS = 64
+
+
+def visiting_order(sizes, sections):
+    arrived = [[[0.0] * len(sizes) if s == 0 and not back else [None] * len(sizes) for back in (0, 1)]
+               for s in range(sections)]
+    clock, link = [0.0] * sections, [[0.0, 0.0] for _ in range(sections)]
+    done, masks = [[0, 0] for _ in range(sections)], [0] * sections
+    while any(count < len(sizes) for pair in done for count in pair):
+        choices = []
+        for s in range(sections):
+            ready = []
+            for back in (1, 0):
+                i = done[s][back]
+                if i < len(sizes) and arrived[s][back][i] is not None:
+                    ready.append((max(clock[s], arrived[s][back][i]), back))
+            if len(ready) == 2 and ready[0][0] > ready[1][0] + 0.0:
+                ready.reverse()
+            if ready:
+                choices.append((ready[0][0], s, ready[0][1]))
+        start, s, back = min(choices)
+        i = done[s][back]
+        spent = 0.1 if back and s == 0 else 1.3 + 0.005 * sizes[i] + 0.15 * back
+        masks[s] |= back << (done[s][0] + done[s][1])
+        done[s][back] += 1
+        clock[s] = start + spent + 0.06
+        wire = 0.09 * sizes[i]
+        link[s][back] = max(max(start + 0.45, link[s][back]) + wire, start + spent + wire / 4)
+        if not back and s + 1 < sections:
+            arrived[s + 1][0][i] = link[s][0] + 1.75
+        if not back and s + 1 == sections:
+            arrived[s][1][i] = clock[s]
+        if back and s > 0:
+            arrived[s - 1][1][i] = link[s][1] + 1.75
+    return masks
+
+
+def early_rows(rows):
+    return max(rows - LATE_ROWS, SMALL * SMALL_COUNT)
 
 
 def fused_fits(mesh, activations, weight):
@@ -168,9 +210,12 @@
         and replicas == 2 * len(HALVES) ** 2
         and sections > 1
         and shard_rows % 128 == 0
-        and rows % 16 == 0
+        and rows % BIG == 0
+        and (SMALL * SMALL_COUNT) % BIG == 0
+        and rows > SMALL * SMALL_COUNT + LATE_ROWS
+        and 2 * (SMALL_COUNT + rows // BIG) < 30
         and width % 512 == 0
-        and gathered + 3 * width * width * 2 < 40 * 2**20
+        and gathered + 5 * width * width * 2 < 56 * 2**20
     )
 
 
@@ -184,11 +229,11 @@
 
 
 def fused_kernel(
-    chunk, tokens, act, cot, weight, gain, pairs_hbm, earlier, out, flips,
-    packed, full, hidden, normed, deriv, outgoing, upstream, downstream, grads, terms,
-    scaled, partial, incoming, counts, pairs, own_pairs, load_sem, row_sem,
+    tokens, act, cot, weight, gain, pairs_hbm, earlier, own_out, sent_out, flips,
+    packed, full, turned, hidden, normed, deriv, preacts, scales, outgoing, upstream, downstream, grads, terms,
+    acc, partial, counts, pairs, own_pairs, load_sem, row_sem,
     pack_send, pack_recv, relay_send, relay_recv, fwd_send, fwd_recv, bwd_send, bwd_recv,
-    term_send, term_recv, grad_send, grad_recv, part_send, part_recv, flip_send, flip_recv, pair_sem,
+    term_send, term_recv, grad_send, pass_recv, last_recv, part_send, part_recv, flip_send, flip_recv, pair_sem, out_sem,
 ):
     section = lax.axis_index("section")
     sections = lax.axis_size("section")
@@ -201,7 +246,10 @@
     shard_rows, width = weight.shape
     groups = shard_rows // 4
     rows = hidden.shape[0]
-    steps = rows // chunk
+    steps = SMALL_COUNT + (rows - SMALL * SMALL_COUNT) // BIG
+    early = early_rows(rows)
+    early_steps = SMALL_COUNT + (early - SMALL * SMALL_COUNT) // BIG
+    halves = (slice(0, early), slice(early, rows))
     tile = 512
     tiles = width // tile
     across = chip + 1 - 2 * lax.rem(chip, 2)
@@ -341,6 +389,19 @@
 
     all_load.wait()
 
+    block = 256
+    same = lax.broadcasted_iota(jnp.int32, (block, block), 0) == lax.broadcasted_iota(jnp.int32, (block, block), 1)
+    unit = jnp.where(same, 1.0, 0.0).astype(jnp.bfloat16)
+
+    def turn(first_owner):
+        source = pl.ds(pl.multiple_of(first_owner * shard_rows, 2 * shard_rows), 2 * shard_rows)
+        for b in range(width // block):
+            cols = slice(b * block, (b + 1) * block)
+            flipped = lax.dot_general(
+                unit, full[source, cols], (((1,), (1,)), ((), ())), preferred_element_type=jnp.float32
+            )
+            turned[cols, source] = flipped.astype(jnp.bfloat16)
+
     def unpack_two(first, second):
         def one(k, carry):
             unpack(jnp.where(k == 0, first, second))
@@ -348,8 +409,21 @@
 
         lax.fori_loop(0, 2, one, 0)
 
+    def turn_some(*owners):
+        @pl.when(section > 0)
+        def _():
+            def one(k, carry):
+                owner = jnp.int32(owners[0])
+                for n in range(1, len(owners)):
+                    owner = jnp.where(k == n, owners[n], owner)
+                turn(owner)
+                return carry
+
+            lax.fori_loop(0, len(owners), one, 0)
+
     relay_copy(chip, 1 - core).wait_recv()
     unpack_two(2 * chip + core, 2 * chip + 1 - core)
+    turn_some(2 * chip)
     for way in (0, 1):
         pack_arrival(near[way], way).wait_recv()
         pack_onward(way).start()
@@ -360,12 +434,14 @@
     for way in (0, 1):
         relay_copy(near[way], 1 - core).wait_recv()
     unpack_two(2 * across + 1 - core, 2 * along_y + 1 - core)
+    turn_some(2 * across, 2 * along_y)
     for h in HALVES:
         pack_arrival(corner, h).wait_recv()
     relay_copy(corner, core).start()
     unpack_two_first = 2 * corner + core
     relay_copy(corner, 1 - core).wait_recv()
     unpack_two(unpack_two_first, 2 * corner + 1 - core)
+    turn_some(2 * corner)
 
     @pl.when(section == 0)
     def _():
@@ -377,165 +453,208 @@
         for load in row_loads(cot, upstream):
             load.wait()
 
-    def span(i):
-        return pl.ds(pl.multiple_of(i * chunk, chunk), chunk)
-
-    def fwd_copy(i):
-        return remote(outgoing.at[span(i)], hidden.at[span(i)], fwd_send.at[i], fwd_recv.at[i], {"section": section + 1})
-
-    def fwd_arrival(i):
-        return remote(outgoing.at[span(i)], hidden.at[span(i)], fwd_send.at[i], fwd_recv.at[i], {"section": section})
-
-    def bwd_copy(i):
-        return remote(downstream.at[span(i)], upstream.at[span(i)], bwd_send.at[i], bwd_recv.at[i], {"section": section - 1})
-
-    def bwd_arrival(i):
-        return remote(downstream.at[span(i)], upstream.at[span(i)], bwd_send.at[i], bwd_recv.at[i], {"section": section})
-
-    def term_copy(k, i):
+    def span(i, size):
+        if size == SMALL:
+            return pl.ds(pl.multiple_of(i * SMALL, SMALL), size)
+        return pl.ds(pl.multiple_of(SMALL * SMALL_COUNT + (i - SMALL_COUNT) * BIG, BIG), size)
+
+    def fwd_copy(where, cols, i, to):
+        return remote(outgoing.at[where, cols], hidden.at[where, cols], fwd_send, fwd_recv.at[i], {"section": to})
+
+    def bwd_copy(where, cols, i, to):
+        return remote(downstream.at[where, cols], upstream.at[where, cols], bwd_send, bwd_recv.at[i], {"section": to})
+
+    everything = slice(0, width)
+
+    def part_of(i):
+        return jnp.where(i >= early_steps, 1, 0)
+
+    def term_copy(k, where, part):
         peer = peer_chip(k)
         wanted = pl.ds(pl.multiple_of(peer * 2 * shard_rows, 2 * shard_rows), 2 * shard_rows)
         return remote(
-            normed.at[span(i), wanted], terms.at[chip, span(i)],
-            term_send.at[k, i], term_recv.at[chip, i], at_dp(2 * peer + core),
+            normed.at[where, wanted], terms.at[chip, where],
+            term_send.at[k], term_recv.at[chip, part], at_dp(2 * peer + core),
         )
 
-    def grad_copy(way, source, h, route, i):
-        slot = grads.at[source, span(i), pl.ds(h * (width // 2), width // 2)]
+    def half_columns(h):
+        return pl.ds(h * (width // 2), width // 2)
+
+    def grad_passed(way, source, where, i):
+        slot = grads.at[source, where, half_columns(way)]
+        return remote(slot, slot, grad_send.at[way, 0], pass_recv.at[way, i], at_dp(2 * near[way] + core))
+
+    def grad_final(way, source, h, route, where, part):
+        slot = grads.at[source, where, half_columns(h)]
         return remote(
-            slot, slot, grad_send.at[route * 2 + h, i], grad_recv.at[source * 2 + h, i], at_dp(2 * near[way] + core)
+            slot, slot, grad_send.at[way, route], last_recv.at[source * 2 + h, part], at_dp(2 * near[way] + core)
         )
 
-    def grad_own(way, h, i):
-        return grad_copy(way, chip, h, way, i)
-
-    def grad_onward(way, i):
-        return grad_copy(1 - way, near[way], way, 2, i)
-
-    def grad_arrival(source, h, i):
-        return grad_copy(0, source, h, 0, i)
-
-    def pass_on(i):
+    def grad_onward(way, where, part):
+        return grad_final(1 - way, near[way], way, 2, where, part)
+
+    def pass_on(i, size):
+        where = span(i, size)
         for way in (0, 1):
-            grad_arrival(near[way], way, i).wait_recv()
-            grad_onward(way, i).start()
-
-    def forward(i):
+            grad_passed(way, near[way], where, i).wait_recv()
+            grad_onward(way, where, part_of(i)).start()
+
+    def filled(block):
+        if block.shape[0] <= SMALL:
+            return block
+        return jnp.concatenate([block] * (FILL // block.shape[0]), axis=0)
+
+    def forward(i, size, sends):
+        where = span(i, size)
+
         @pl.when(section > 0)
         def _():
-            fwd_arrival(i).wait_recv()
-
-        values = hidden[span(i)].astype(jnp.float32)
+            fwd_copy(where, everything, i, section).wait_recv()
+
+        values = hidden[where].astype(jnp.float32)
+        lifted = values * gain[...]
+        ready = lifted.astype(jnp.bfloat16)
         scale = lax.rsqrt(jnp.mean(values * values, axis=-1, keepdims=True) + epsilon)
-        rounded = (values * scale * gain[...]).astype(jnp.bfloat16)
-        normed[span(i)] = rounded
-        for t in range(tiles):
-            cols = slice(t * tile, (t + 1) * tile)
-            preact = jnp.dot(rounded, full[:, cols], preferred_element_type=jnp.float32)
+        scales[where] = jnp.broadcast_to(scale, (size, 128))
+        column_tiles = [slice(t * tile, (t + 1) * tile) for t in range(tiles)]
+
+        streamed = filled(ready)
+
+        def multiply(cols):
+            return jnp.dot(streamed, full[:, cols], preferred_element_type=jnp.float32)[:size]
+
+        later = multiply(column_tiles[0])
+        for t, cols in enumerate(column_tiles):
+            preact = scale * later
+            if t + 1 < tiles:
+                later = multiply(column_tiles[t + 1])
             cdf = 0.5 * (1.0 + lax.erf(preact * half_root))
             pdf = jnp.exp(-0.5 * preact * preact) * density_scale
-            deriv[span(i), cols] = cdf + preact * pdf
-            outgoing[span(i), cols] = (values[:, cols] + preact * cdf).astype(jnp.bfloat16)
+            preacts[where, cols] = preact
+            deriv[where, cols] = cdf + preact * pdf
+            if sends:
+                outgoing[where, cols] = (values[:, cols] + preact * cdf).astype(jnp.bfloat16)
+                fwd_copy(where, cols, i, section + 1).start()
+        normed[where] = (lifted * scale).astype(jnp.bfloat16)
+        terms[chip, where] = normed[where, pl.ds(own_columns, 2 * shard_rows)]
+        for k in range(1, chips):
+            term_copy(k, where, part_of(i)).start()
+
+    def backward(i, size, sends):
+        where = span(i, size)
 
         @pl.when(section < last)
         def _():
-            fwd_copy(i).start()
-
-        terms[chip, span(i)] = normed[span(i), pl.ds(own_columns, 2 * shard_rows)]
-        for k in range(1, chips):
-            term_copy(k, i).start()
-
-    lag = min(2, steps)
-
-    def backward(i):
-        @pl.when(section < last)
-        def _():
-            bwd_arrival(i).wait_recv()
-
-        above = upstream[span(i)].astype(jnp.float32)
-        grad_pre = (above * deriv[span(i)]).astype(jnp.bfloat16)
-        grads[chip, span(i)] = grad_pre
-        for h in HALVES:
-            for way in (0, 1):
-                grad_own(way, h if way == 0 else 1 - h, i).start()
-
-        @pl.when(i >= lag)
-        def _():
-            pass_on(i - lag)
-
-        @pl.when(section > 0)
-        def _():
-            values = hidden[span(i)].astype(jnp.float32)
-            scale = lax.rsqrt(jnp.mean(values * values, axis=-1, keepdims=True) + epsilon)
-            along = jnp.zeros((chunk, 1), jnp.float32)
-            for t in range(tiles):
-                cols = slice(t * tile, (t + 1) * tile)
-                piece = lax.dot_general(
-                    grad_pre, full[cols, :], (((1,), (1,)), ((), ())), preferred_element_type=jnp.float32
-                ) * gain[:, cols]
-                scaled[:, cols] = piece
-                along = along + jnp.sum(piece * values[:, cols], axis=-1, keepdims=True)
-            pull = scale * scale * scale * (along / width)
-            result = upstream[span(i)].astype(jnp.float32) + scale * scaled[...] - values * pull
-            downstream[span(i)] = result.astype(jnp.bfloat16)
-            bwd_copy(i).start()
+            bwd_copy(where, everything, i, section).wait_recv()
+
+        above = upstream[where].astype(jnp.float32)
+        slope = above * deriv[where]
+        grad_pre = slope.astype(jnp.bfloat16)
+        grads[chip, where] = grad_pre
+        if sends:
+            scale = scales[where, 0:1]
+            along = jnp.sum(slope * preacts[where], axis=-1, keepdims=True)
+            pull = scale * scale * (along / width)
+            column_tiles = [slice(t * tile, (t + 1) * tile) for t in range(tiles)]
+
+            streamed = filled(grad_pre)
+
+            def multiply(cols):
+                return jnp.dot(streamed, turned[:, cols], preferred_element_type=jnp.float32)[:size]
+
+            later = multiply(column_tiles[0])
+            for t, cols in enumerate(column_tiles):
+                piece = later * gain[:, cols]
+                if t + 1 < tiles:
+                    later = multiply(column_tiles[t + 1])
+                result = (
+                    upstream[where, cols].astype(jnp.float32)
+                    + scale * piece
+                    - hidden[where, cols].astype(jnp.float32) * pull
+                )
+                downstream[where, cols] = result.astype(jnp.bfloat16)
+                bwd_copy(where, cols, i, section - 1).start()
+        for way in (0, 1):
+            grad_passed(way, chip, where, i).start()
+        for way in (0, 1):
+            grad_final(way, chip, 1 - way, 1, where, part_of(i)).start()
+
+    def by_size(i, action):
+        @pl.when(i < SMALL_COUNT)
+        def _():
+            action(i, SMALL)
+
+        @pl.when(i >= SMALL_COUNT)
+        def _():
+            action(i, BIG)
+
+    lag = jnp.where(section == 0, 1, min(FAR_LAG, steps - SMALL_COUNT))
+    sizes = [SMALL] * SMALL_COUNT + [BIG] * (steps - SMALL_COUNT)
+    order = jnp.int32(0)
+    for s, mask in enumerate(visiting_order(sizes, sections)):
+        order = jnp.where(section == s, mask, order)
 
     def step(k, carry):
-        at_last = (section == last).astype(jnp.int32)
-        half = lax.div(k, 2)
-        goes_back = at_last * lax.rem(k, 2) + (1 - at_last) * lax.div(k, steps)
-        index = at_last * half + (1 - at_last) * lax.rem(k, steps)
-
-        @pl.when(goes_back == 0)
-        def _():
-            forward(index)
-
-        @pl.when(goes_back == 1)
-        def _():
-            backward(index)
-
-        return carry
-
-    lax.fori_loop(0, 2 * steps, step, 0)
-
-    def arrivals(i, carry):
+        left, forwards = carry
+        back_bit = lax.rem(left, 2)
+        goes_back = back_bit == 1
+        index = jnp.where(goes_back, k - forwards, forwards)
+
+        @pl.when(jnp.logical_not(goes_back) & (section < last))
+        def _():
+            by_size(index, lambda i, size: forward(i, size, True))
+
+        @pl.when(jnp.logical_not(goes_back) & (section == last))
+        def _():
+            by_size(index, lambda i, size: forward(i, size, False))
+
+        @pl.when(goes_back & (section > 0))
+        def _():
+            by_size(index, lambda i, size: backward(i, size, True))
+
+        @pl.when(goes_back & (section == 0))
+        def _():
+            by_size(index, lambda i, size: backward(i, size, False))
+
+        @pl.when(goes_back & (index >= lag))
+        def _():
+            by_size(index - lag, pass_on)
+
+        return lax.div(left, 2), forwards + 1 - back_bit
+
+    lax.fori_loop(0, 2 * steps, step, (order, jnp.int32(0)))
+
+    def arrivals(part):
+        where = halves[part]
         for k in range(1, chips):
             source = peer_chip(k)
-            remote(
-                terms.at[source, span(i)], terms.at[source, span(i)],
-                term_send.at[k, i], term_recv.at[source, i], at_dp(me),
-            ).wait_recv()
+            slot = terms.at[source, where]
+            remote(slot, slot, term_send.at[k], term_recv.at[source, part], at_dp(2 * peer_chip(k) + core)).wait_recv()
         for way in (0, 1):
-            grad_arrival(near[way], 1 - way, i).wait_recv()
+            grad_final(way, near[way], 1 - way, 1, where, part).wait_recv()
         for h in HALVES:
-            grad_arrival(corner, h, i).wait_recv()
+            grad_final(0, corner, h, 2, where, part).wait_recv()
+
+    def product(half, cols, part):
+        left = pl.ds(pl.multiple_of(half * shard_rows, shard_rows), shard_rows)
+        rows_of = halves[part]
+        total = jnp.zeros((shard_rows, tile), jnp.float32)
+        if part == 0:
+            for c in range(chips):
+                total = total + lax.dot_general(
+                    terms[c, rows_of, left], grads[c, rows_of, cols],
+                    (((0,), (0,)), ((), ())), preferred_element_type=jnp.float32,
+                )
+            return total
+        stacked = [jnp.concatenate([ref[c, rows_of, which] for c in range(chips)], axis=0)
+                   for ref, which in ((terms, left), (grads, cols))]
+        return lax.dot_general(
+            stacked[0], stacked[1], (((0,), (0,)), ((), ())), preferred_element_type=jnp.float32
+        )
+
+    def pass_rest(i, carry):
+        pass_on(i, BIG)
         return carry
-
-    for i in range(steps - lag, steps):
-        pass_on(i)
-
-    lax.fori_loop(0, steps, arrivals, 0)
-
-    def product(half, cols):
-        left = pl.ds(pl.multiple_of(half * shard_rows, shard_rows), shard_rows)
-        total = jnp.zeros((shard_rows, tile), jnp.float32)
-        for c in range(chips):
-            total = total + lax.dot_general(
-                terms[c, :, left], grads[c, :, cols], (((0,), (0,)), ((), ())), preferred_element_type=jnp.float32
-            )
-        return total
-
-    def part_copy(t):
-        return remote(partial.at[t], incoming.at[t], part_send.at[t], part_recv.at[t], at_dp(sibling))
-
-    for t in range(tiles):
-        partial[t] = product(1 - core, slice(t * tile, (t + 1) * tile)).astype(jnp.bfloat16)
-        part_copy(t).start()
-    own_rows = pl.ds(pl.multiple_of(me * shard_rows, shard_rows), shard_rows)
-    for t in range(tiles):
-        cols = slice(t * tile, (t + 1) * tile)
-        pruned = weight[:, cols].astype(jnp.float32) - full[own_rows, cols].astype(jnp.float32)
-        out[:, cols] = product(core, cols) * (1.0 / math.sqrt(tokens)) + decay_rate * pruned
 
     for k in range(1, chips):
         flip_copy(k, peer_chip(k)).wait_recv()
@@ -545,17 +664,42 @@
     counts[chips] = total
     pair_copy = remote(counts.at[chips], counts.at[chips + 1], pair_sem.at[0], pair_sem.at[1], at_dp(sibling))
     pair_copy.start()
-
+    lax.fori_loop(steps - lag, steps, pass_rest, 0)
+    pair_copy.wait()
+    flips[0] = jnp.sum(counts[chips] + counts[chips + 1])
+    arrivals(0)
     for t in range(tiles):
         cols = slice(t * tile, (t + 1) * tile)
-        part_copy(t).wait_recv()
-        out[:, cols] = out[:, cols] + incoming[t].astype(jnp.float32) * (1.0 / math.sqrt(tokens))
-    pair_copy.wait_recv()
-    flips[...] = counts[chips] + counts[chips + 1]
-
-    pair_copy.wait_send()
+        for side in (0, 1):
+            acc[side, :, cols] = product(jnp.where(side == 0, 1 - core, core), cols, 0)
+    arrivals(1)
+
+    def part_copy(t):
+        return remote(
+            partial.at[t], sent_out.at[:, pl.ds(t * tile, tile)], part_send, part_recv, at_dp(sibling)
+        )
+
+    def own_copy(t):
+        cols = pl.ds(t * tile, tile)
+        return pltpu.make_async_copy(acc.at[1, :, cols], own_out.at[:, cols], out_sem.at[t])
+
     for t in range(tiles):
-        part_copy(t).wait_send()
+        cols = slice(t * tile, (t + 1) * tile)
+        partial[t] = (acc[0, :, cols] + product(1 - core, cols, 1)).astype(jnp.bfloat16)
+        part_copy(t).start()
+    own_rows = pl.ds(pl.multiple_of(me * shard_rows, shard_rows), shard_rows)
+    for t in range(tiles):
+        cols = slice(t * tile, (t + 1) * tile)
+        pruned = weight[:, cols].astype(jnp.float32) - full[own_rows, cols].astype(jnp.float32)
+        dense = acc[1, :, cols] + product(core, cols, 1)
+        acc[1, :, cols] = dense * (1.0 / math.sqrt(tokens)) + decay_rate * pruned
+        own_copy(t).start()
+
+    everything_sent = remote(partial, partial, part_send, part_recv, at_dp(sibling))
+    for t in range(tiles):
+        own_copy(t).wait()
+    everything_sent.wait_recv()
+    everything_sent.wait_send()
     for k in range(1, chips):
         flip_copy(k, chip).wait_send()
 
@@ -566,25 +710,23 @@
     for c in range(chips):
         relay_copy(c, core).wait_send()
 
-    def drain(i, carry):
-        for k in range(1, chips):
-            term_copy(k, i).wait_send()
-        for way in (0, 1):
-            grad_onward(way, i).wait_send()
-            for h in HALVES:
-                grad_own(way, h, i).wait_send()
-
-        @pl.when(section < last)
-        def _():
-            fwd_copy(i).wait_send()
-
-        @pl.when(section > 0)
-        def _():
-            bwd_copy(i).wait_send()
-
-        return carry
-
-    lax.fori_loop(0, steps, drain, 0)
+    whole = slice(0, rows)
+    for k in range(1, chips):
+        term_copy(k, whole, 0).wait_send()
+    for way in (0, 1):
+        slot = grads.at[chip, whole, half_columns(way)]
+        for route in (0, 1, 2):
+            remote(
+                slot, slot, grad_send.at[way, route], last_recv.at[0, 0], at_dp(2 * near[way] + core)
+            ).wait_send()
+
+    @pl.when(section < last)
+    def _():
+        fwd_copy(whole, everything, 0, section + 1).wait_send()
+
+    @pl.when(section > 0)
+    def _():
+        bwd_copy(whole, everything, 0, section - 1).wait_send()
 
 
 def fused_body(activations, cotangent, weight, norm_gain, pair_mask, earlier_mask):
@@ -594,44 +736,46 @@
     shard_rows = weight.shape[1]
     groups = shard_rows // 4
     rows = micro * micro_rows
-    chunk = pick_chunk(rows)
-    steps = rows // chunk
+    steps = SMALL_COUNT + (rows - SMALL * SMALL_COUNT) // BIG
     tile = 512
     tiles = width // tile
     bf, f32 = jnp.bfloat16, jnp.float32
     dma = pltpu.SemaphoreType.DMA
     vmem = pl.BlockSpec(memory_space=pltpu.VMEM)
     hbm = pl.BlockSpec(memory_space=pl.ANY)
-    gradient, flips = pl.pallas_call(
-        functools.partial(fused_kernel, chunk, rows * replicas),
+    own, sent, flips = pl.pallas_call(
+        functools.partial(fused_kernel, rows * replicas),
         out_shape=(
             jax.ShapeDtypeStruct((shard_rows, width), f32),
-            jax.ShapeDtypeStruct((8, 128), jnp.int32),
+            jax.ShapeDtypeStruct((shard_rows, width), bf),
+            jax.ShapeDtypeStruct((1,), jnp.int32),
         ),
         in_specs=[hbm, hbm, vmem, vmem, hbm, vmem],
-        out_specs=(vmem, vmem),
+        out_specs=(hbm, hbm, pl.BlockSpec(memory_space=pltpu.SMEM)),
         scratch_shapes=[
             pltpu.VMEM((replicas, 2 * groups, width), bf),
+            pltpu.VMEM((width, width), bf),
             pltpu.VMEM((width, width), bf),
             pltpu.VMEM((rows, width), bf),
             pltpu.VMEM((rows, width), bf),
             pltpu.VMEM((rows, width), f32),
+            pltpu.VMEM((rows, width), f32),
+            pltpu.VMEM((rows, 128), f32),
             pltpu.VMEM((rows, width), bf),
             pltpu.VMEM((rows, width), bf),
             pltpu.VMEM((rows, width), bf),
             pltpu.VMEM((chips, rows, width), bf),
             pltpu.VMEM((chips, rows, 2 * shard_rows), bf),
-            pltpu.VMEM((chunk, width), f32),
-            pltpu.VMEM((tiles, shard_rows, tile), bf),
+            pltpu.VMEM((2, shard_rows, width), f32),
             pltpu.VMEM((tiles, shard_rows, tile), bf),
             pltpu.VMEM((chips + 2, 8, 128), jnp.int32),
             pltpu.VMEM((width // 4, width), jnp.int32),
             pltpu.VMEM((groups, width), jnp.int32),
             dma((2,)), dma((micro,)),
             dma((3, 2)), dma((chips, 2)), dma((chips,)), dma((chips,)),
-            dma((steps,)), dma((steps,)), dma((steps,)), dma((steps,)),
-            dma((chips, steps)), dma((chips, steps)), dma((6, steps)), dma((2 * chips, steps)),
-            dma((tiles,)), dma((tiles,)), dma((chips,)), dma((chips,)), dma((2,)),
+            dma, dma((steps,)), dma, dma((steps,)),
+            dma((chips,)), dma((chips, 2)), dma((2, 3)), dma((2, steps)), dma((2 * chips, 2)),
+            dma, dma, dma((chips,)), dma((chips,)), dma((2,)), dma((tiles,)),
         ],
         compiler_params=pltpu.CompilerParams(
             collective_id=0, has_side_effects=True, vmem_limit_bytes=60 * 2**20
@@ -640,7 +784,8 @@
     )(
         activations, cotangent, weight[0], norm_gain, pair_mask[0], earlier_mask[0],
     )
-    return (gradient[None], jnp.sum(flips).reshape(1))
+    gradient = own + sent.astype(f32) * (1.0 / math.sqrt(rows * replicas))
+    return (gradient[None], flips)
 
 
 def solution(mesh):

time: 124 us -> 105 us (0.85)
  Pallas kernels: 119 us -> 98.4 us
  local copies, waits for them, and re-layouts: 3.13 us -> 0 us
  other arithmetic: 1.32 us -> 3.56 us
  between operations: 0.64 us -> 2.39 us
    pallas_call x1, Pallas kernels: 119 us -> 98.4 us  [fused_body(): pl.pallas_call(functools.partial(fused_kernel, rows * replicas), out_shap...]
    broadcast_in_dim x0 -> x1, other arithmetic: none -> 3.56 us  [fused_body(): return (gradient[None], flips)]
    unnamed x1 -> x0, local copies, waits for them, and re-layouts: 3.13 us -> none
    reduce_sum x1 -> x0, other arithmetic: 1.32 us -> none  [fused_body(): return (gradient[None], jnp.sum(flips).reshape(1))]
where the time goes in v1:
time: 105 us; the launch traced here: 104 us
  Pallas kernels  98.4 us (94%)
  other arithmetic  3.56 us (3%)
  between operations  2.39 us (2%)
    pallas_call x1, Pallas kernels, fused_body(): pl.pallas_call(functools.partial(fused_kernel, rows * replicas), out_shap...  98.4 us
    broadcast_in_dim x1, other arithmetic, fused_body(): return (gradient[None], flips)  3.56 us

profile of v1, /device:TPU:0, one launch (start us, length us, event | category | flops | bytes accessed | tf_op | source)
XLA Modules:
  0.0 104.4 jit_solution(16965823735458363131)
XLA Ops:
  0.6 98.4 %fused_step.1 = (f32[256,2048]{1,0:T(8,128)}, bf16[256,2048]{1,0:T(8,128)(2,1)}, s32[1]{0:T(128)}) custom-call(bf16[4,64,2048]{2,1,0:T(8,128)(2,1)} %act.1, bf16[4,64,2048]{2,1,0:T(8,128)(2,1)} %cot.1, bf16[256,2048]{1,0:T(8,128)(2,1)} %bitcast.6, f32[1,2048]{1,0:T(1,128)} %gain.1, s32[512,2048]{1,0:T(8,128)} %bitcast.5, s32[64,2048]{1,0:T(8,128)} %bitcast.7), custom_call_target="tpu_custom_call" | custom-call | tf_op jit(solution)/shard_map/fused_step/pallas_call | solution.py:746
  99.0 3.6 %add_bitcast_fusion = f32[1,256,2048]{2,1,0:T(8,128)} fusion(f32[256,2048]{1,0:T(8,128)} %get-tuple-element.5, bf16[256,2048]{1,0:T(8,128)(2,1)} %get-tuple-element.6), kind=kLoop, calls=%fused_computation | loop fusion | flops 1572864 | bytes 5242880 | tf_op jit(solution)/shard_map/broadcast_in_dim | solution.py:788
